TPU v7x, 128 devices: a whole 4x4x4 slice. The times are simulated.
128 devices in a mesh: grp: 8 (over z, core), brick: 16 (over x, y).
Axes of the slice: x: 4, y: 4, z: 4, core: 2. Of those that a mesh axis runs over, the one named last changes fastest.
Arguments:
- noisy: float32 [128, 64, 4096], P(('grp', 'brick')), may hold values from -6 to 6
- neighbours: int32 [128, 6], P(('grp', 'brick')), may hold values from -1 to 127, as said below
- labels: int32 [8, 16], P('grp'), may hold values from 0 to 2
- conv_in: float32 [64, 1728], replicated, may hold values from -0.15625 to 0.15625
- bias_in: float32 [64], replicated, may hold values from -3 to 3
- down_fine: float32 [128, 64], replicated, may hold values from -0.75 to 0.75
- conv_mid: float32 [128, 3456], replicated, may hold values from -0.109375 to 0.109375
- bias_mid: float32 [128], replicated, may hold values from -3 to 3
- conv_res: float32 [128, 3456], replicated, may hold values from -0.109375 to 0.109375
- conv_dec: float32 [128, 3456], replicated, may hold values from -0.109375 to 0.109375
- down_mid: float32 [256, 128], replicated, may hold values from -0.5 to 0.5
- w_query: float32 [256, 256], replicated, may hold values from -0.375 to 0.375
- w_key: float32 [256, 256], replicated, may hold values from -0.375 to 0.375
- w_value: float32 [256, 256], replicated, may hold values from -0.375 to 0.375
- w_out: float32 [256, 256], replicated, may hold values from -0.375 to 0.375
- logit_scale: float32 [4], replicated, may hold values from 1 to 40, as said below
- up_mid: float32 [128, 256], replicated, may hold values from -0.375 to 0.375
- up_fine: float32 [64, 128], replicated, may hold values from -0.5 to 0.5
- conv_out: float32 [64, 1728], replicated, may hold values from -0.15625 to 0.15625
Outputs:
- noise_pred: float32 [128, 64, 4096], P(('grp', 'brick'))
Inputs may be any that keep to these rules, and one draw needn't show every extreme that they name: `neighbours`: row i lists, for faces -x, +x, -y, +y, -z, +z, the brick whose position touches brick i there, or -1. Where row i names j at face f, row j names i at face f xor 1. Bricks are numbered in Morton order of their positions. `logit_scale`: positive factors.
All inputs are finite; a program needn't handle non-finite values.
Results may differ from a plain program's by a relative error of at most 0.0003.
Values sent between devices are 32-bit elements; how exact they have to be, the bound alone decides.
No kernel may reach another device: no remote copies, remote signals or barrier semaphores. Data moves between devices by JAX's collectives and lax.ppermute only.
A program may use at most 192 MiB of HBM per device.

v0:
```python
import jax
import jax.numpy as jnp
from jax import lax
from jax.sharding import PartitionSpec as P

S = 16
C1 = 64
C2 = 128
C3 = 256
HEADS = 4
HDIM = 64
TOKB = 64


HIGHEST = lax.Precision.HIGHEST
EPSILON = 1e-06


def in_order(parts, dim):
    shape = list(parts.shape[1:])
    shape[dim] *= parts.shape[0]
    return jnp.moveaxis(parts, 0, dim).reshape(shape)


def copy_for_each(shard, axis):
    size = lax.axis_size(axis)
    return lax.all_to_all(
        jnp.broadcast_to(shard[None], (size, *shard.shape)), axis, 0, 0, tiled=True
    )


def gathered_copies(shard, axis, dim):
    return in_order(copy_for_each(shard, axis), dim)


def face_layers(brick_block):
    channels = brick_block.shape[0]
    edge_len = brick_block.shape[1]
    sheets = [
        brick_block[:, 0],
        brick_block[:, -1],
        brick_block[:, :, 0],
        brick_block[:, :, -1],
        brick_block[:, :, :, 0],
        brick_block[:, :, :, -1],
    ]
    return jnp.stack([one_sheet.reshape(channels, edge_len * edge_len) for one_sheet in sheets])


def padded_block(brick_block, halo_faces):
    channels = brick_block.shape[0]
    edge_len = brick_block.shape[1]
    sheets = halo_faces.reshape(6, channels, edge_len, edge_len)
    padded = jnp.pad(brick_block, ((0, 0), (1, 1), (1, 1), (1, 1)))
    padded = padded.at[:, 0, 1:-1, 1:-1].set(sheets[0])
    padded = padded.at[:, -1, 1:-1, 1:-1].set(sheets[1])
    padded = padded.at[:, 1:-1, 0, 1:-1].set(sheets[2])
    padded = padded.at[:, 1:-1, -1, 1:-1].set(sheets[3])
    padded = padded.at[:, 1:-1, 1:-1, 0].set(sheets[4])
    padded = padded.at[:, 1:-1, 1:-1, -1].set(sheets[5])
    return padded


def convolve(padded, weight):
    channels = padded.shape[0]
    edge_len = padded.shape[1] - 2
    voxels = edge_len**3
    summed = jnp.zeros((weight.shape[0], voxels), jnp.float32)
    for along_x in range(3):
        shifted = [
            padded[
                :,
                along_x : along_x + edge_len,
                along_y : along_y + edge_len,
                along_z : along_z + edge_len,
            ].reshape(channels, voxels)
            for along_y in range(3)
            for along_z in range(3)
        ]
        stacked = jnp.concatenate(shifted, axis=0)
        weight_part = weight[:, along_x * 9 * channels : (along_x + 1) * 9 * channels]
        summed = summed + jnp.dot(
            weight_part, stacked, precision=HIGHEST, preferred_element_type=jnp.float32
        )
    return summed


def pooled(brick_block):
    channels = brick_block.shape[0]
    halved = brick_block.shape[1] // 2
    return brick_block.reshape(channels, halved, 2, halved, 2, halved, 2).mean(axis=(2, 4, 6))


def widened(brick_block):
    channels = brick_block.shape[0]
    edge_len = brick_block.shape[1]
    spread = jnp.broadcast_to(
        brick_block[:, :, None, :, None, :, None], (channels, edge_len, 2, edge_len, 2, edge_len, 2)
    )
    return spread.reshape(channels, 2 * edge_len, 2 * edge_len, 2 * edge_len)


def head_norm(values):
    return values * lax.rsqrt(jnp.mean(values * values, axis=-1, keepdims=True) + EPSILON)


def fetch_halo(face_sheets, face_links, coarse):
    device_count = lax.axis_size(("grp", "brick"))
    owners = lax.broadcasted_iota(jnp.int32, (device_count, 6), 0)
    outgoing = (face_links[None, :] == owners).astype(jnp.float32)
    parcel = jnp.einsum("ng,gcv->ncv", outgoing, face_sheets, precision=HIGHEST)
    if coarse:
        arrived = lax.all_to_all(parcel, ("grp", "brick"), split_axis=0, concat_axis=0, tiled=True)
    else:
        arrived = lax.all_to_all(parcel, ("grp", "brick"), split_axis=0, concat_axis=0, tiled=True)
    halo_faces = jnp.einsum("ng,ncv->gcv", outgoing, arrived, precision=HIGHEST)
    return halo_faces


def brick_conv(brick_block, face_links, weight, coarse):
    halo_faces = fetch_halo(face_layers(brick_block), face_links, coarse)
    return convolve(padded_block(brick_block, halo_faces), weight)


def group_attention(tokens, group_labels, w_query, w_key, w_value, w_out, logit_scale):
    members = group_labels.shape[0]
    normed = head_norm(tokens)
    query_rows = head_norm(jnp.dot(normed, w_query, precision=HIGHEST).reshape(TOKB, HEADS, HDIM))
    head_scale = logit_scale / jnp.sqrt(jnp.float32(HDIM))
    position = lax.axis_index("brick")
    member_ids = lax.iota(jnp.int32, members)
    own_label = jnp.sum(jnp.where(member_ids == position, group_labels, 0))
    piece = gathered_copies(normed, "brick", 0)
    key_part = jnp.dot(piece, w_key, precision=HIGHEST)
    row_peak = jnp.full((HEADS, TOKB), -1e30, jnp.float32)
    part_rows = key_part.shape[0]
    brick_ids = lax.iota(jnp.int32, part_rows) // TOKB
    key_labels = jnp.sum(
        jnp.where(brick_ids[:, None] == member_ids[None, :], group_labels[None, :], 0), axis=1
    )
    allowed = key_labels == own_label
    key_heads = head_norm(key_part.reshape(part_rows, HEADS, HDIM))
    logits = (
        jnp.einsum("qhd,khd->hqk", query_rows, key_heads, precision=HIGHEST)
        * head_scale[:, None, None]
    )
    logits = jnp.where(allowed[None, None, :], logits, -1e30)
    new_peak = jnp.maximum(row_peak, jnp.max(logits, axis=-1))
    exponent = jnp.where(allowed[None, None, :], jnp.exp(logits - new_peak[:, :, None]), 0.0)
    summed = jnp.sum(exponent, axis=-1)
    gathered = jnp.einsum(
        "hqk,khd->hqd",
        exponent,
        jnp.dot(piece, w_value, precision=HIGHEST).reshape(part_rows, HEADS, HDIM),
        precision=HIGHEST,
    )
    out_heads = gathered / summed[:, :, None]
    attended = jnp.transpose(out_heads, (1, 0, 2)).reshape(TOKB, C3)
    return tokens + jnp.dot(attended, w_out, precision=HIGHEST)


def per_device(
    noisy,
    neighbours,
    labels,
    conv_in,
    bias_in,
    down_fine,
    conv_mid,
    bias_mid,
    conv_res,
    conv_dec,
    down_mid,
    w_query,
    w_key,
    w_value,
    w_out,
    logit_scale,
    up_mid,
    up_fine,
    conv_out,
):
    face_links = neighbours[0]
    half_edge = S // 2
    quarter = S // 4
    fine_block = noisy[0].reshape(C1, S, S, S)
    first_level = jax.nn.silu(brick_conv(fine_block, face_links, conv_in, False) + bias_in[:, None])
    shrunk = pooled(first_level.reshape(C1, S, S, S)).reshape(C1, half_edge**3)
    mid_in = jnp.dot(down_fine, shrunk, precision=HIGHEST, preferred_element_type=jnp.float32)
    second = jax.nn.silu(
        brick_conv(mid_in.reshape(C2, half_edge, half_edge, half_edge), face_links, conv_mid, True)
        + bias_mid[:, None]
    )
    refined = second + jax.nn.silu(
        brick_conv(second.reshape(C2, half_edge, half_edge, half_edge), face_links, conv_res, True)
    )
    coarse = pooled(refined.reshape(C2, half_edge, half_edge, half_edge)).reshape(C2, TOKB)
    tokens = lax.dot_general(coarse, down_mid, (((0,), (1,)), ((), ())), precision=HIGHEST)
    mixed = group_attention(tokens, labels[0], w_query, w_key, w_value, w_out, logit_scale)
    lifted = lax.dot_general(up_mid, mixed, (((1,), (1,)), ((), ())), precision=HIGHEST).reshape(
        C2, quarter, quarter, quarter
    )
    joined = refined + widened(lifted).reshape(C2, half_edge**3)
    decoded = jax.nn.silu(
        brick_conv(joined.reshape(C2, half_edge, half_edge, half_edge), face_links, conv_dec, True)
    )
    dropped = jnp.dot(
        up_fine, decoded, precision=HIGHEST, preferred_element_type=jnp.float32
    ).reshape(C1, half_edge, half_edge, half_edge)
    fine_mix = jax.nn.silu(first_level + widened(dropped).reshape(C1, S**3))
    result = brick_conv(fine_mix.reshape(C1, S, S, S), face_links, conv_out, False)
    return result.reshape(1, C1, S**3)


def solution(mesh):
    in_specs = (
        P(("grp", "brick"), None, None),
        P(("grp", "brick"), None),
        P("grp", None),
        P(),
        P(),
        P(),
        P(),
        P(),
        P(),
        P(),
        P(),
        P(),
        P(),
        P(),
        P(),
        P(),
        P(),
        P(),
        P(),
    )
    out_specs = P(("grp", "brick"), None, None)
    return jax.shard_map(
        per_device, mesh=mesh, in_specs=in_specs, out_specs=out_specs, check_vma=False
    )
```

profile of v0, /device:TPU:1, one launch (start us, length us, event | category | flops | bytes accessed | tf_op | source)
XLA Modules:
  0.0 840.0 jit_solution(17584309704976479323)
XLA Ops:
  15.0 12.3 %all-to-all-start = ((f32[128,64,256]{2,1,0:T(8,128)}), f32[128,64,256]{2,1,0:T(8,128)}, u32[]{:S(2)}, u32[]{:S(2)}) async-start(f32[128,64,256]{2,1,0:T(8,128)} %copy.220), calls=%async_computation | async-start | bytes 16777216 | tf_op jit(solution)/shard_map/all_to_all | solution.py:115
  29.6 97.3 %all-to-all-done = f32[128,64,256]{2,1,0:T(8,128)} async-done(((f32[128,64,256]{2,1,0:T(8,128)}), f32[128,64,256]{2,1,0:T(8,128)}, u32[]{:S(2)}, u32[]{:S(2)}) %all-to-all-start) | async-done | bytes 8388640 | tf_op jit(solution)/shard_map/all_to_all | solution.py:115
  126.9 10.5 %fusion.2 = f32[6,64,256]{2,0,1:T(8,128)S(1)} fusion(f32[128,64,256]{2,1,0:T(8,128)} %all-to-all-done, s32[6]{0:T(128)S(1)} %bitcast.565), kind=kOutput, calls=%fused_computation.2 | convolution fusion | flops 150995712 | bytes 8781848 | tf_op jit(solution)/shard_map/ng,ncv->gcv/dot_general | solution.py:116
  154.1 30.0 %fusion.90 = (f32[64,16,16,16]{0,3,2,1:T(8,128)}, f32[64,16,16,16]{0,3,2,1:T(8,128)}, f32[64,16,16,16]{0,3,2,1:T(8,128)}, f32[64,16,16,16]{0,3,2,1:T(8,128)}, f3...) fusion(f32[64,18,18,18]{0,3,2,1:T(8,128)} %scatter.109), kind=kLoop, calls=%fused_computation.197 | loop fusion | bytes 39845888 | tf_op jit(solution)/shard_map/slice | solution.py:71
  190.0 16.4 %concatenate.123 = f32[576,4096]{0,1:T(8,128)} concatenate(f32[64,4096]{0,1:T(8,128)} %bitcast.392, f32[64,4096]{0,1:T(8,128)} %bitcast.391, f32[64,4096]{0,1:T(8,128)} %bitcast.390, f32[64,4096]{0,1:T(8,128)} %bitcast.389, f32[64,4096]{0,1:T(8,128)} %bitcast.388, f32[64,4096]{0,1:T(8,128)} %bitcast.387, f32[64,4096]{0,1:T(8,128)} %bitcast.386, f32[64,4096]{0,1:T(8,128)} %bitcast.385, ...), dimensions={0} | concatenate | bytes 18874368 | tf_op jit(solution)/shard_map/concatenate | solution.py:80
  206.4 13.3 %fusion.52 = f32[4096,64]{0,1:T(8,128)S(1)} fusion(f32[576,4096]{0,1:T(8,128)} %concatenate.123, f32[64,1728]{1,0:T(8,128)} %param.82), kind=kOutput, calls=%fused_computation.149 | convolution fusion | flops 1811939328 | bytes 11698176 | tf_op jit(solution)/shard_map/dot_general | solution.py:82
  219.7 15.9 %concatenate.124 = f32[576,4096]{0,1:T(8,128)} concatenate(f32[64,4096]{0,1:T(8,128)} %bitcast.373, f32[64,4096]{0,1:T(8,128)} %bitcast.372, f32[64,4096]{0,1:T(8,128)} %bitcast.371, f32[64,4096]{0,1:T(8,128)} %bitcast.370, f32[64,4096]{0,1:T(8,128)} %bitcast.369, f32[64,4096]{0,1:T(8,128)} %bitcast.368, f32[64,4096]{0,1:T(8,128)} %bitcast.367, f32[64,4096]{0,1:T(8,128)} %bitcast.366, ...), dimensions={0} | concatenate | bytes 18874368 | tf_op jit(solution)/shard_map/concatenate | solution.py:80
  235.7 13.1 %convolution_add_fusion.3 = f32[4096,64]{0,1:T(8,128)S(1)} fusion(f32[4096,64]{0,1:T(8,128)S(1)} %fusion.52, f32[576,4096]{0,1:T(8,128)} %concatenate.124, f32[64,1728]{1,0:T(8,128)} %param.82), kind=kOutput, calls=%fused_computation.10 | convolution fusion | flops 1812201472 | bytes 12746752 | tf_op jit(solution)/shard_map/dot_general | solution.py:82
  248.8 16.4 %concatenate.125 = f32[576,4096]{0,1:T(8,128)} concatenate(f32[64,4096]{0,1:T(8,128)} %bitcast.355, f32[64,4096]{0,1:T(8,128)} %bitcast.354, f32[64,4096]{0,1:T(8,128)} %bitcast.353, f32[64,4096]{0,1:T(8,128)} %bitcast.352, f32[64,4096]{0,1:T(8,128)} %bitcast.351, f32[64,4096]{0,1:T(8,128)} %bitcast.350, f32[64,4096]{0,1:T(8,128)} %bitcast.349, f32[64,4096]{0,1:T(8,128)} %bitcast.348, ...), dimensions={0} | concatenate | bytes 18874368 | tf_op jit(solution)/shard_map/concatenate | solution.py:80
  265.2 13.7 %divide_multiply_fusion.1 = f32[64,4096]{1,0:T(8,128)S(1)} fusion(f32[4096,64]{0,1:T(8,128)S(1)} %convolution_add_fusion.3, f32[576,4096]{0,1:T(8,128)} %concatenate.125, f32[64]{0:T(128)S(1)} %copy-done.16, f32[64,1728]{1,0:T(8,128)} %param.82), kind=kOutput, calls=%fused_computation.37 | convolution fusion | flops 1813512192 | bytes 12747008 | tf_op jit(solution)/shard_map/dot_general | solution.py:82
  291.0 10.0 %all-to-all-start.1 = ((f32[128,128,64]{1,2,0:T(8,128)}), f32[128,128,64]{1,2,0:T(8,128)}, u32[]{:S(2)}, u32[]{:S(2)}) async-start(f32[128,128,64]{1,2,0:T(8,128)} %copy.233), calls=%async_computation.1 | async-start | bytes 8388608 | tf_op jit(solution)/shard_map/all_to_all | solution.py:113
  301.2 52.2 %all-to-all-done.1 = f32[128,128,64]{1,2,0:T(8,128)} async-done(((f32[128,128,64]{1,2,0:T(8,128)}), f32[128,128,64]{1,2,0:T(8,128)}, u32[]{:S(2)}, u32[]{:S(2)}) %all-to-all-start.1) | async-done | bytes 4194336 | tf_op jit(solution)/shard_map/all_to_all | solution.py:113
  383.9 49.6 %all-to-all-done.2 = f32[128,128,64]{1,2,0:T(8,128)} async-done(((f32[128,128,64]{1,2,0:T(8,128)}), f32[128,128,64]{1,2,0:T(8,128)}, u32[]{:S(2)}, u32[]{:S(2)}) %all-to-all-start.2) | async-done | bytes 4194336 | tf_op jit(solution)/shard_map/all_to_all | solution.py:113
  455.6 14.9 %all-to-all-done.3 = f32[16,64,256]{2,1,0:T(8,128)S(1)} async-done(((f32[16,64,256]{2,1,0:T(8,128)}), f32[16,64,256]{2,1,0:T(8,128)S(1)}, u32[]{:S(2)}, u32[]{:S(2)}) %all-to-all-start.3) | async-done | bytes 1048608 | tf_op jit(solution)/shard_map/all_to_all | solution.py:27
  491.1 52.2 %all-to-all-done.4 = f32[128,128,64]{1,2,0:T(8,128)} async-done(((f32[128,128,64]{1,2,0:T(8,128)}), f32[128,128,64]{1,2,0:T(8,128)}, u32[]{:S(2)}, u32[]{:S(2)}) %all-to-all-start.4) | async-done | bytes 4194336 | tf_op jit(solution)/shard_map/all_to_all | solution.py:113
  587.8 97.3 %all-to-all-done.5 = f32[128,64,256]{2,1,0:T(8,128)} async-done(((f32[128,64,256]{2,1,0:T(8,128)}), f32[128,64,256]{2,1,0:T(8,128)}, u32[]{:S(2)}, u32[]{:S(2)}) %all-to-all-start.5) | async-done | bytes 8388640 | tf_op jit(solution)/shard_map/all_to_all | solution.py:115
  685.1 10.5 %fusion = f32[6,64,256]{2,0,1:T(8,128)S(1)} fusion(f32[128,64,256]{2,1,0:T(8,128)} %all-to-all-done.5, s32[6]{0:T(128)S(1)} %bitcast.573), kind=kOutput, calls=%fused_computation | convolution fusion | flops 150995712 | bytes 8781848 | tf_op jit(solution)/shard_map/ng,ncv->gcv/dot_general | solution.py:116
  712.3 30.0 %fusion.88 = (f32[64,16,16,16]{0,3,2,1:T(8,128)}, f32[64,16,16,16]{0,3,2,1:T(8,128)}, f32[64,16,16,16]{0,3,2,1:T(8,128)}, f32[64,16,16,16]{0,3,2,1:T(8,128)}, f3...) fusion(f32[64,18,18,18]{0,3,2,1:T(8,128)} %scatter.149), kind=kLoop, calls=%fused_computation.195 | loop fusion | bytes 39845888 | tf_op jit(solution)/shard_map/slice | solution.py:71
  748.2 16.0 %concatenate.135 = f32[576,4096]{0,1:T(8,128)} concatenate(f32[64,4096]{0,1:T(8,128)} %bitcast.400, f32[64,4096]{0,1:T(8,128)} %bitcast.399, f32[64,4096]{0,1:T(8,128)} %bitcast.398, f32[64,4096]{0,1:T(8,128)} %bitcast.397, f32[64,4096]{0,1:T(8,128)} %bitcast.396, f32[64,4096]{0,1:T(8,128)} %bitcast.395, f32[64,4096]{0,1:T(8,128)} %bitcast.394, f32[64,4096]{0,1:T(8,128)} %bitcast.393, ...), dimensions={0} | concatenate | bytes 18874368 | tf_op jit(solution)/shard_map/concatenate | solution.py:80
  764.2 13.4 %fusion.48 = f32[4096,64]{0,1:T(8,128)S(1)} fusion(f32[576,4096]{0,1:T(8,128)} %concatenate.135, f32[64,1728]{1,0:T(8,128)S(1)} %copy-done.8), kind=kOutput, calls=%fused_computation.145 | convolution fusion | flops 1811939328 | bytes 10649600 | tf_op jit(solution)/shard_map/dot_general | solution.py:82
  777.6 16.4 %concatenate.136 = f32[576,4096]{0,1:T(8,128)} concatenate(f32[64,4096]{0,1:T(8,128)} %bitcast.382, f32[64,4096]{0,1:T(8,128)} %bitcast.381, f32[64,4096]{0,1:T(8,128)} %bitcast.380, f32[64,4096]{0,1:T(8,128)} %bitcast.379, f32[64,4096]{0,1:T(8,128)} %bitcast.378, f32[64,4096]{0,1:T(8,128)} %bitcast.377, f32[64,4096]{0,1:T(8,128)} %bitcast.376, f32[64,4096]{0,1:T(8,128)} %bitcast.375, ...), dimensions={0} | concatenate | bytes 18874368 | tf_op jit(solution)/shard_map/concatenate | solution.py:80
  793.9 13.1 %convolution_add_fusion.1 = f32[4096,64]{0,1:T(8,128)S(1)} fusion(f32[4096,64]{0,1:T(8,128)S(1)} %fusion.48, f32[576,4096]{0,1:T(8,128)} %concatenate.136, f32[64,1728]{1,0:T(8,128)S(1)} %copy-done.8), kind=kOutput, calls=%fused_computation.6 | convolution fusion | flops 1812201472 | bytes 11698176 | tf_op jit(solution)/shard_map/dot_general | solution.py:82
  807.1 16.4 %concatenate.137 = f32[576,4096]{0,1:T(8,128)} concatenate(f32[64,4096]{0,1:T(8,128)} %bitcast.364, f32[64,4096]{0,1:T(8,128)} %bitcast.363, f32[64,4096]{0,1:T(8,128)} %bitcast.362, f32[64,4096]{0,1:T(8,128)} %bitcast.361, f32[64,4096]{0,1:T(8,128)} %bitcast.360, f32[64,4096]{0,1:T(8,128)} %bitcast.359, f32[64,4096]{0,1:T(8,128)} %bitcast.358, f32[64,4096]{0,1:T(8,128)} %bitcast.357, ...), dimensions={0} | concatenate | bytes 18874368 | tf_op jit(solution)/shard_map/concatenate | solution.py:80
  823.5 16.2 %fusion.4 = f32[1,64,4096]{2,1,0:T(8,128)} fusion(f32[4096,64]{0,1:T(8,128)S(1)} %convolution_add_fusion.1, f32[576,4096]{0,1:T(8,128)} %concatenate.137, f32[64,1728]{1,0:T(8,128)S(1)} %copy-done.8), kind=kOutput, calls=%fused_computation.5 | convolution fusion | flops 1812201472 | bytes 11698176 | tf_op jit(solution)/shard_map/dot_general | solution.py:82
  (283 shorter events, 190.6 us)
Async XLA Ops:
  0.0 454.9 %copy-start = (f32[256,256]{1,0:T(8,128)S(1)}, f32[256,256]{1,0:T(8,128)}, u32[]{:S(2)}) copy-start(f32[256,256]{1,0:T(8,128)} %param.90) | copy-start | bytes 786436
  1.9 1.5 copy-start.14
  15.0 111.9 %all-to-all-start = ((f32[128,64,256]{2,1,0:T(8,128)}), f32[128,64,256]{2,1,0:T(8,128)}, u32[]{:S(2)}, u32[]{:S(2)}) async-start(f32[128,64,256]{2,1,0:T(8,128)} %copy.220), calls=%async_computation | async-start | bytes 16777216 | tf_op jit(solution)/shard_map/all_to_all | solution.py:115
  154.1 30.0 %copy-start.3 = (f32[64,18,18,18]{0,3,2,1:T(8,128)S(1)}, f32[64,18,18,18]{0,3,2,1:T(8,128)}, u32[]{:S(2)}) copy-start(f32[64,18,18,18]{0,3,2,1:T(8,128)} %scatter.109) | copy-start | bytes 4478980
  248.8 16.4 %copy-start.16 = (f32[64]{0:T(128)S(1)}, f32[64]{0:T(128)}, u32[]{:S(2)}) copy-start(f32[64]{0:T(128)} %param.83) | copy-start | bytes 772
  278.9 5.0 copy-start.15
  291.0 62.4 %all-to-all-start.1 = ((f32[128,128,64]{1,2,0:T(8,128)}), f32[128,128,64]{1,2,0:T(8,128)}, u32[]{:S(2)}, u32[]{:S(2)}) async-start(f32[128,128,64]{1,2,0:T(8,128)} %copy.233), calls=%async_computation.1 | async-start | bytes 8388608 | tf_op jit(solution)/shard_map/all_to_all | solution.py:113
  365.2 2.1 copy-start.17
  376.5 4.9 copy-start.10
  376.6 5.8 copy-start.11
  376.6 5.9 copy-start.18
  376.6 57.0 %all-to-all-start.2 = ((f32[128,128,64]{1,2,0:T(8,128)}), f32[128,128,64]{1,2,0:T(8,128)}, u32[]{:S(2)}, u32[]{:S(2)}) async-start(f32[128,128,64]{1,2,0:T(8,128)} %copy.239), calls=%async_computation.2 | async-start | bytes 8388608 | tf_op jit(solution)/shard_map/all_to_all | solution.py:113
  447.2 2.3 copy-start.12
  449.3 5.6 copy-start.20
  449.5 21.0 %copy-start.7 = (f32[256,256]{0,1:T(8,128)S(1)}, f32[256,256]{0,1:T(8,128)}, u32[]{:S(2)}) copy-start(f32[256,256]{0,1:T(8,128)} %copy.247) | copy-start | bytes 786436
  451.0 19.4 %all-to-all-start.3 = ((f32[16,64,256]{2,1,0:T(8,128)}), f32[16,64,256]{2,1,0:T(8,128)S(1)}, u32[]{:S(2)}, u32[]{:S(2)}) async-start(f32[16,64,256]{2,1,0:T(8,128)} %broadcast_in_dim.76), calls=%async_computation.3 | async-start | bytes 2097152 | tf_op jit(solution)/shard_map/all_to_all | solution.py:27
  473.8 1.9 copy-start.9
  473.8 2.1 copy-start.13
  483.1 60.2 %all-to-all-start.4 = ((f32[128,128,64]{1,2,0:T(8,128)}), f32[128,128,64]{1,2,0:T(8,128)}, u32[]{:S(2)}, u32[]{:S(2)}) async-start(f32[128,128,64]{1,2,0:T(8,128)} %copy.251), calls=%async_computation.4 | async-start | bytes 8388608 | tf_op jit(solution)/shard_map/all_to_all | solution.py:113
  556.9 2.1 copy-start.19
  580.5 104.6 %all-to-all-start.5 = ((f32[128,64,256]{2,1,0:T(8,128)}), f32[128,64,256]{2,1,0:T(8,128)}, u32[]{:S(2)}, u32[]{:S(2)}) async-start(f32[128,64,256]{2,1,0:T(8,128)} %copy.266), calls=%async_computation.5 | async-start | bytes 16777216 | tf_op jit(solution)/shard_map/all_to_all | solution.py:115
  712.3 30.0 %copy-start.2 = (f32[64,18,18,18]{0,3,2,1:T(8,128)S(1)}, f32[64,18,18,18]{0,3,2,1:T(8,128)}, u32[]{:S(2)}) copy-start(f32[64,18,18,18]{0,3,2,1:T(8,128)} %scatter.149) | copy-start | bytes 4478980
  748.2 16.0 %copy-start.8 = (f32[64,1728]{1,0:T(8,128)S(1)}, f32[64,1728]{1,0:T(8,128)}, u32[]{:S(2)}) copy-start(f32[64,1728]{1,0:T(8,128)} %param.97) | copy-start | bytes 1327108
  823.5 16.2 %copy-start.1 = (f32[256,256]{1,0:T(8,128)S(1)}, f32[256,256]{1,0:T(8,128)}, u32[]{:S(2)}) copy-start(f32[256,256]{1,0:T(8,128)} %param.90) | copy-start | bytes 786436
  (3 other events, 4.4 us)
where the time goes:
time: 854 us; the launch traced here: 840 us
  waiting for transfers between devices  364 us (43%)
  local copies, waits for them, and re-layouts  265 us (31%)
  matrix products  159 us (19%)
  starting transfers between devices  44 us (5%)
    all_to_all x5, waiting for transfers between devices, fetch_halo(): lax.all_to_all(parcel, ('grp', 'brick'), split_axis=0, concat_axis=0, til...  349 us
    dot_general x15, matrix products, convolve(): jnp.dot(weight_part, stacked, precision=HIGHEST, preferred_element_type=j...  102 us
    concatenate x15, local copies, waits for them, and re-layouts, convolve(): stacked = jnp.concatenate(shifted, axis=0)  97.7 us
    slice x10, local copies, waits for them, and re-layouts, convolve(): padded[:, along_x:along_x + edge_len, along_y:along_y + edge_len, along_z...  73.7 us
    all_to_all x5, starting transfers between devices, fetch_halo(): lax.all_to_all(parcel, ('grp', 'brick'), split_axis=0, concat_axis=0, til...  40.2 us
    dot_general x5, matrix products, fetch_halo(): halo_faces = jnp.einsum('ng,ncv->gcv', outgoing, arrived, precision=HIGHEST)  38.4 us
    dot_general x5, local copies, waits for them, and re-layouts, fetch_halo(): parcel = jnp.einsum('ng,gcv->ncv', outgoing, face_sheets, precision=HIGHEST)  30 us
  transfers between devices with their start and end apart: 6, of which 6 were waited for; matrix products, arithmetic and copies ran while one was open for 1% of the time, Pallas kernels for 0%

commit v1 on v0

v1 whole, which is shorter than its diff:
```python
import jax
import jax.numpy as jnp
from jax import lax
from jax.experimental import pallas as pl
from jax.experimental.pallas import tpu as pltpu
from jax.sharding import PartitionSpec as P

S = 16
C1 = 64
C2 = 128
C3 = 256
HEADS = 4
HDIM = 64
TOKB = 64
BRICKS = 128
GROUPS = 8
MEMBERS = 16
SLOTS_B = 2
SLOTS_G = 3
FROM_B = 6
FROM_G = FROM_B + MEMBERS * SLOTS_B
FROM_X = FROM_G + GROUPS * SLOTS_G
EPSILON = 1e-06
ALL = ("grp", "brick")

f32 = jnp.float32
bf16 = jnp.bfloat16


def split(v):
    hi = v.astype(bf16)
    return hi, (v - hi.astype(f32)).astype(bf16)


def mm(a, b, nt=False):
    return lax.dot_general(
        a, b, (((1,), (1 if nt else 0,)), ((), ())), preferred_element_type=f32
    )


def dot3(a, b, nt=False):
    rows = a.shape[0]
    ah, al = split(a)
    bh, bl = split(b)
    both = mm(jnp.concatenate([ah, al], axis=0), bh, nt)
    return both[:rows] + both[rows:] + mm(ah, bl, nt)


def dot2(a, selector, nt=False):
    rows = a.shape[0]
    ah, al = split(a)
    both = mm(jnp.concatenate([ah, al], axis=0), selector, nt)
    return both[:rows] + both[rows:]


def iota(shape, dim):
    return lax.broadcasted_iota(jnp.int32, shape, dim)


def as01(mask):
    return jnp.where(mask, 1.0, 0.0).astype(bf16)


def silu(v):
    return v / (1.0 + jnp.exp(-v))


def lane_roll(v, shift):
    amount = shift % v.shape[1]
    return v if amount == 0 else pltpu.roll(v, amount, 1)


def in_range(index, edge):
    return (index >= 0) & (index < edge)


def face_taps(face):
    side = 2 * (face % 2)
    if face < 2:
        return [9 * side + 3 * a + b for a in range(3) for b in range(3)]
    if face < 4:
        return [9 * a + 3 * side + b for a in range(3) for b in range(3)]
    return [9 * a + 3 * b + side for a in range(3) for b in range(3)]


def tap_columns(w_ref, taps, channels):
    runs = []
    for t in taps:
        if runs and runs[-1][1] == t:
            runs[-1][1] = t + 1
        else:
            runs.append([t, t + 1])
    pieces = [w_ref[:, lo * channels : hi * channels] for lo, hi in runs]
    return pieces[0] if len(pieces) == 1 else jnp.concatenate(pieces, axis=1)


def coarse_edges():
    row = iota((384, 512), 0)
    col = iota((384, 512), 1)
    pair = row >> 7
    edge = ((row >> 6) & 1) * 7
    a = (row >> 3) & 7
    b = row & 7
    x = col >> 6
    y = (col >> 3) & 7
    z = col & 7
    along = jnp.where(pair == 0, x, jnp.where(pair == 1, y, z))
    first = jnp.where(pair == 0, y, x)
    last = jnp.where(pair == 2, y, z)
    return as01((along == edge) & (first == a) & (last == b))


def fine_sides():
    row = iota((256, 256), 0)
    col = iota((256, 256), 1)
    edge = (row >> 7) * 15
    return as01(((col & 15) == edge) & ((col >> 4) == (row & 15)))


def fine_sides_t():
    row = iota((256, 256), 0)
    col = iota((256, 256), 1)
    edge = (col >> 7) * 15
    return as01(((row & 15) == edge) & ((row >> 4) == (col & 15)))


def send_faces(faces_ref, send_ref, slot_ref, sems):
    def copy(face):
        return pltpu.make_async_copy(
            faces_ref.at[face], send_ref.at[slot_ref[face]], sems.at[face]
        )

    for face in range(6):

        @pl.when(slot_ref[face] >= 0)
        def _():
            copy(face).start()

    for face in range(6):

        @pl.when(slot_ref[face] >= 0)
        def _():
            copy(face).wait()


def fetch_halo(pools, bounds, index_ref, halo_ref, sems):
    def each(act):
        for face in range(6):
            source = index_ref[face]
            for pool, low, high in zip(pools, bounds[:-1], bounds[1:]):

                @pl.when((source >= low) & (source < high))
                def _():
                    copy = pltpu.make_async_copy(
                        pool.at[source - low], halo_ref.at[face], sems.at[face]
                    )
                    act(copy)

    each(lambda copy: copy.start())
    for face in range(6):

        @pl.when(index_ref[face] < 0)
        def _():
            halo_ref[face] = jnp.zeros(halo_ref.shape[1:], f32)

    each(lambda copy: copy.wait())


def coarse_faces(v, edges, faces_ref):
    rows = v.shape[0] // 2
    picked = dot2(v, edges, nt=True)
    low = iota((rows, 128), 1) < 64
    for pair in range(3):
        block = picked[:, pair * 128 : (pair + 1) * 128]
        top = block[:rows]
        bottom = block[rows:]
        faces_ref[2 * pair] = jnp.where(low, top, pltpu.roll(bottom, 64, 1))
        faces_ref[2 * pair + 1] = jnp.where(low, pltpu.roll(top, 64, 1), bottom)


def fine_faces(v_ref, faces_ref):
    faces_ref[0] = v_ref[:, 0:256]
    faces_ref[1] = v_ref[:, 3840:4096]
    sides = fine_sides_t()
    at_x = iota((C1, 128), 1) >> 4
    for half in range(2):
        found = [None] * 4
        for k in range(8):
            start = (half * 8 + k) * 256
            part = v_ref[:, start : start + 256]
            near = dot2(part, sides)
            new = [
                lane_roll(part[:, :128], 16 * k),
                lane_roll(part[:, 128:], 16 * k - 112),
                near[:, :128],
                near[:, 128:],
            ]
            if k == 0:
                found = new
            else:
                found = [jnp.where(at_x == k, n, o) for n, o in zip(new, found)]
        for kind in range(4):
            faces_ref[2 + kind, :, half * 128 : (half + 1) * 128] = found[kind]


def route_kernel(table_ref, me_ref, slot_ref, relay_ref, final_ref):
    g = me_ref[0]
    b = me_ref[1]
    me = g * MEMBERS + b

    def rank_b(i, face, member):
        count = jnp.int32(0)
        for other in range(5):
            j = table_ref[i * 6 + other]
            hit = (j >= 0) & ((j & 15) == member) & (other < face)
            count = count + jnp.where(hit, 1, 0)
        return count

    def rank_g(j, face, group):
        count = jnp.int32(0)
        for other in range(face):
            i = table_ref[j * 6 + other]
            hit = (i >= 0) & ((i >> 4) == group)
            count = count + jnp.where(hit, 1, 0)
        return count

    for face in range(6):
        j = table_ref[me * 6 + face]
        member = j & 15
        rank = rank_b(me, face, member)
        fine = (j >= 0) & (member != b) & (rank < SLOTS_B)
        slot_ref[face] = jnp.where(fine, member * SLOTS_B + rank, -1)
    for slot in range(GROUPS * SLOTS_G):
        relay_ref[slot] = jnp.int32(-1)

    def relay_to(group, carry):
        j = group * MEMBERS + b
        for face in range(6):
            i = table_ref[j * 6 + face]
            mine = (i >= 0) & ((i >> 4) == g) & (group != g)
            safe = jnp.maximum(i, 0)
            rank = rank_g(j, face, g)
            first = rank_b(safe, face ^ 1, b)
            member = safe & 15
            source = jnp.where(
                member == b, face ^ 1, FROM_B + member * SLOTS_B + first
            )
            fits = mine & (rank < SLOTS_G) & ((member == b) | (first < SLOTS_B))

            @pl.when(fits)
            def _():
                relay_ref[group * SLOTS_G + rank] = source

        return carry

    lax.fori_loop(0, GROUPS, relay_to, 0)
    for face in range(6):
        i = table_ref[me * 6 + face]
        safe = jnp.maximum(i, 0)
        first = jnp.minimum(rank_b(safe, face ^ 1, b), SLOTS_B - 1)
        group = safe >> 4
        rank = jnp.minimum(rank_g(me, face, group), SLOTS_G - 1)
        source = jnp.where(
            group == g,
            FROM_B + (safe & 15) * SLOTS_B + first,
            FROM_G + group * SLOTS_G + rank,
        )
        final_ref[face] = jnp.where(i >= 0, source, -1)


def relay_kernel(faces_ref, recv_ref, index_ref, out_ref, sems):
    def each(act):
        def one(slot, carry):
            source = index_ref[slot]

            @pl.when((source >= 0) & (source < FROM_B))
            def _():
                act(pltpu.make_async_copy(faces_ref.at[source], out_ref.at[slot], sems.at[slot]))

            @pl.when(source >= FROM_B)
            def _():
                act(
                    pltpu.make_async_copy(
                        recv_ref.at[source - FROM_B], out_ref.at[slot], sems.at[slot]
                    )
                )

            return carry

        lax.fori_loop(0, GROUPS * SLOTS_G, one, 0)

    each(lambda copy: copy.start())
    each(lambda copy: copy.wait())


def fine_face_kernel(v_ref, faces_ref):
    fine_faces(v_ref, faces_ref)


def pack_kernel(faces_ref, slot_ref, send_ref, sems):
    send_faces(faces_ref, send_ref, slot_ref, sems)


def split_weights(w_ref, stacked_ref):
    rows = w_ref.shape[0]
    hi, lo = split(w_ref[...])
    stacked_ref[0:rows, :] = hi
    stacked_ref[rows : 2 * rows, :] = lo


def fine_conv_kernel(v_ref, w_ref, out_ref, hi_ref, lo_ref, stacked_ref):
    split_weights(w_ref, stacked_ref)
    for ref in (hi_ref, lo_ref):
        ref[:, 0:256] = jnp.zeros((576, 256), bf16)
        ref[:, 4352:4608] = jnp.zeros((576, 256), bf16)
    lane = iota((C1, 256), 1)
    y = lane >> 4
    z = lane & 15

    def plane(x, carry):
        part = v_ref[:, pl.ds(pl.multiple_of(x * 256, 256), 256)]
        for tap in range(9):
            dy, dz = tap // 3 - 1, tap % 3 - 1
            moved = lane_roll(part, -(16 * dy + dz))
            keep = in_range(y + dy, S) & in_range(z + dz, S)
            hi, lo = split(jnp.where(keep, moved, 0.0))
            at = pl.ds(pl.multiple_of(x * 256 + 256, 256), 256)
            hi_ref[tap * C1 : (tap + 1) * C1, at] = hi
            lo_ref[tap * C1 : (tap + 1) * C1, at] = lo
        return carry

    lax.fori_loop(0, S, plane, 0)

    def block(n, carry):
        def gathered(ref):
            return jnp.concatenate(
                [
                    ref[:, pl.ds(pl.multiple_of(n * 512 + dx * 256, 256), 512)]
                    for dx in range(3)
                ],
                axis=0,
            )

        both = mm(stacked_ref[...], gathered(hi_ref))
        low = mm(stacked_ref[0:C1, :], gathered(lo_ref))
        at = pl.ds(pl.multiple_of(n * 512, 512), 512)
        out_ref[:, at] = both[:C1] + both[C1:] + low
        return carry

    lax.fori_loop(0, 8, block, 0)


def fine_halo(acc_ref, halo_ref, w_ref, out_ref):
    lane = iota((C1, 256), 1)
    a = lane >> 4
    b = lane & 15
    sheets = []
    for face in range(6):
        layer = halo_ref[face]
        his, los = [], []
        for tap in range(9):
            da, db = tap // 3 - 1, tap % 3 - 1
            keep = in_range(a + da, S) & in_range(b + db, S)
            moved = lane_roll(layer, -(16 * da + db))
            hi, lo = split(jnp.where(keep, moved, 0.0))
            his.append(hi)
            los.append(lo)
        wh, wl = split(tap_columns(w_ref, face_taps(face), C1))
        both = mm(jnp.concatenate([wh, wl], axis=0), jnp.concatenate(his, axis=0))
        low = mm(wh, jnp.concatenate(los, axis=0))
        sheets.append(both[:C1] + both[C1:] + low)
    sides = fine_sides()
    at_x = (iota((2 * C1, 256), 1) >> 4) & 7
    lane = iota((C1, 128), 1)
    for half in range(2):
        at = slice(half * 128, (half + 1) * 128)
        near = jnp.concatenate([sheets[4][:, at], sheets[5][:, at]], axis=1)
        hi, lo = split(near)
        spread = jnp.concatenate([hi, lo], axis=0)
        for k in range(8):
            x = half * 8 + k
            both = mm(spread * as01(at_x == k), sides)
            start = x * 256
            total = acc_ref[:, start : start + 256] + both[:C1] + both[C1:]
            low = lane_roll(sheets[2][:, at], -16 * k)
            high = lane_roll(sheets[3][:, at], 112 - 16 * k)
            ends = jnp.concatenate(
                [jnp.where(lane < 16, low, 0.0), jnp.where(lane >= 112, high, 0.0)], axis=1
            )
            total = total + ends
            if x == 0:
                total = total + sheets[0]
            if x == S - 1:
                total = total + sheets[1]
            out_ref[:, start : start + 256] = total


def fine_last_kernel(acc_ref, w_ref, recv_ref, relayed_ref, extra_ref, final_ref, out_ref, halo_ref, sems):
    fetch_halo(
        [recv_ref, relayed_ref, extra_ref], [FROM_B, FROM_G, FROM_X, FROM_X + 6], final_ref, halo_ref, sems
    )
    fine_halo(acc_ref, halo_ref, w_ref, out_ref)


def fine_first_kernel(
    acc_ref,
    w_ref,
    bias_ref,
    down_ref,
    recv_ref,
    relayed_ref,
    extra_ref,
    final_ref,
    links_ref,
    first_ref,
    mid_ref,
    send_ref,
    halo_ref,
    faces_ref,
    sems,
):
    fetch_halo(
        [recv_ref, relayed_ref, extra_ref], [FROM_B, FROM_G, FROM_X, FROM_X + 6], final_ref, halo_ref, sems
    )
    fine_halo(acc_ref, halo_ref, w_ref, first_ref)
    first_ref[...] = silu(first_ref[...] + bias_ref[...])
    row = iota((512, 128), 0)
    col = iota((512, 128), 1)
    target = (row >> 8) * 64 + ((row >> 5) & 7) * 8 + ((row >> 1) & 7)
    pool = jnp.where(target == col, 0.125, 0.0).astype(bf16)
    parts = []
    for quad in range(4):
        planes = [
            first_ref[:, (4 * quad + k) * 256 : (4 * quad + k + 1) * 256] for k in range(4)
        ]
        pair = jnp.concatenate([planes[0] + planes[1], planes[2] + planes[3]], axis=1)
        parts.append(dot2(pair, pool))
    shrunk = jnp.concatenate(parts, axis=1)
    mid_ref[...] = dot3(down_ref[...], shrunk)
    coarse_faces(shrunk, coarse_edges(), faces_ref)
    send_faces(faces_ref, send_ref, links_ref, sems)


def coarse_conv_kernel(v_ref, w_ref, out_ref, hi_ref, lo_ref, stacked_ref):
    split_weights(w_ref, stacked_ref)
    lane = iota((16, 512), 1)
    x = lane >> 6
    y = (lane >> 3) & 7
    z = lane & 7

    def chunk(n, carry):
        part = v_ref[pl.ds(pl.multiple_of(n * 16, 16), 16), :]
        for tap in range(27):
            dx, dy, dz = tap // 9 - 1, tap // 3 % 3 - 1, tap % 3 - 1
            keep = in_range(x + dx, 8) & in_range(y + dy, 8) & in_range(z + dz, 8)
            moved = lane_roll(part, -(64 * dx + 8 * dy + dz))
            hi, lo = split(jnp.where(keep, moved, 0.0))
            at = pl.ds(pl.multiple_of(tap * C2 + n * 16, 16), 16)
            hi_ref[at, :] = hi
            lo_ref[at, :] = lo
        return carry

    lax.fori_loop(0, C2 // 16, chunk, 0)

    def block(n, carry):
        at = pl.ds(pl.multiple_of(n * 256, 256), 256)
        both = mm(stacked_ref[...], hi_ref[:, at])
        low = mm(stacked_ref[0:C2, :], lo_ref[:, at])
        out_ref[:, at] = both[:C2] + both[C2:] + low
        return carry

    lax.fori_loop(0, 2, block, 0)


def coarse_halo(acc_ref, halo_ref, w_ref, edges, down=None):
    rows = halo_ref.shape[1]
    low_lane = iota((rows, 128), 1) < 64
    lane = iota((C2, 128), 1)
    a = (lane >> 3) & 7
    b = lane & 7
    sheets = []
    for pair in range(3):
        even = halo_ref[2 * pair]
        odd = halo_ref[2 * pair + 1]
        top = jnp.where(low_lane, even, pltpu.roll(odd, 64, 1))
        bottom = jnp.where(low_lane, pltpu.roll(even, 64, 1), odd)
        layer = jnp.concatenate([top, bottom], axis=0)
        if down is not None:
            layer = dot3(down, layer)
        his, los = [], []
        for tap in range(9):
            da, db = tap // 3 - 1, tap % 3 - 1
            keep = in_range(a + da, 8) & in_range(b + db, 8)
            moved = lane_roll(layer, -(8 * da + db))
            hi, lo = split(jnp.where(keep, moved, 0.0))
            his.append(hi)
            los.append(lo)
        eh, el = split(tap_columns(w_ref, face_taps(2 * pair), C2))
        oh, ol = split(tap_columns(w_ref, face_taps(2 * pair + 1), C2))
        both = mm(jnp.concatenate([eh, el, oh, ol], axis=0), jnp.concatenate(his, axis=0))
        low = mm(jnp.concatenate([eh, oh], axis=0), jnp.concatenate(los, axis=0))
        even_sum = both[0:C2] + both[C2 : 2 * C2] + low[0:C2]
        odd_sum = both[2 * C2 : 3 * C2] + both[3 * C2 :] + low[C2:]
        sheets.append(jnp.where(lane < 64, even_sum, odd_sum))
    return acc_ref[...] + dot2(jnp.concatenate(sheets, axis=1), edges)


def second_kernel(
    acc_ref,
    w_ref,
    bias_ref,
    down_ref,
    arrived_ref,
    links_ref,
    slot_ref,
    second_ref,
    faces_ref,
    send_ref,
    halo_ref,
    sems,
):
    fetch_halo([arrived_ref], [0, BRICKS], links_ref, halo_ref, sems)
    edges = coarse_edges()
    summed = coarse_halo(acc_ref, halo_ref, w_ref, edges, down_ref[...])
    second = silu(summed + bias_ref[...])
    second_ref[...] = second
    coarse_faces(second, edges, faces_ref)
    send_faces(faces_ref, send_ref, slot_ref, sems)


def pool_rows(scale):
    row = iota((64, 512), 0)
    col = iota((64, 512), 1)
    target = (col >> 7) * 16 + ((col >> 4) & 3) * 4 + ((col >> 1) & 3)
    return jnp.where(target == row, scale, 0.0).astype(bf16)


def refined_kernel(
    acc_ref,
    w_ref,
    second_ref,
    recv_ref,
    relayed_ref,
    extra_ref,
    final_ref,
    refined_ref,
    coarse_ref,
    halo_ref,
    sems,
):
    fetch_halo(
        [recv_ref, relayed_ref, extra_ref], [FROM_B, FROM_G, FROM_X, FROM_X + 6], final_ref, halo_ref, sems
    )
    summed = coarse_halo(acc_ref, halo_ref, w_ref, coarse_edges())
    refined = second_ref[...] + silu(summed)
    refined_ref[...] = refined
    pool = pool_rows(0.125)
    hi, lo = split(refined)
    coarse_ref[...] = mm(pool, hi, nt=True) + mm(pool, lo, nt=True)


def attention_kernel(
    all_ref,
    own_ref,
    refined_ref,
    down_ref,
    wq_ref,
    wk_ref,
    wv_ref,
    wo_ref,
    up_ref,
    scale_ref,
    labels_ref,
    me_ref,
    slot_ref,
    joined_ref,
    faces_ref,
    send_ref,
    sems,
):
    head_of = iota((C3, C3), 1) >> 6
    head_mean = jnp.where((iota((C3, C3), 0) >> 6) == head_of, 1.0 / HDIM, 0.0).astype(bf16)

    def normed(v):
        return v * lax.rsqrt(jnp.mean(v * v, axis=-1, keepdims=True) + EPSILON)

    def head_normed(v):
        return v * lax.rsqrt(dot2(v * v, head_mean) + EPSILON)

    tokens = dot3(own_ref[...], down_ref[...], nt=True)
    query = head_normed(dot3(normed(tokens), wq_ref[...]))
    everyone = normed(dot3(all_ref[...], down_ref[...], nt=True))
    keys = head_normed(dot3(everyone, wk_ref[...]))
    values = dot3(everyone, wv_ref[...])
    lane_head = iota((TOKB, C3), 1) >> 6
    stacked = jnp.concatenate(
        [
            jnp.where(lane_head == h, query, 0.0) * (scale_ref[h] * (HDIM**-0.5))
            for h in range(HEADS)
        ],
        axis=0,
    )
    logits = dot3(stacked, keys, nt=True)
    brick_of = iota((1, MEMBERS * TOKB), 1) >> 6
    key_label = jnp.zeros((1, MEMBERS * TOKB), jnp.int32)
    for member in range(MEMBERS):
        key_label = jnp.where(brick_of == member, labels_ref[member], key_label)
    allowed = key_label == labels_ref[me_ref[1]]
    logits = jnp.where(allowed, logits, -1e30)
    peak = jnp.max(logits, axis=-1, keepdims=True)
    weight = jnp.where(allowed, jnp.exp(logits - peak), 0.0)
    total = jnp.sum(weight, axis=-1, keepdims=True)
    heads = dot3(weight, values) / total
    attended = jnp.zeros((TOKB, C3), f32)
    for h in range(HEADS):
        attended = jnp.where(lane_head == h, heads[h * TOKB : (h + 1) * TOKB], attended)
    mixed = tokens + dot3(attended, wo_ref[...])
    lifted = dot3(up_ref[...], mixed, nt=True)
    joined = refined_ref[...] + dot2(lifted, pool_rows(1.0))
    joined_ref[...] = joined
    coarse_faces(joined, coarse_edges(), faces_ref)
    send_faces(faces_ref, send_ref, slot_ref, sems)


def decoded_kernel(
    acc_ref,
    w_ref,
    up_ref,
    first_ref,
    recv_ref,
    relayed_ref,
    extra_ref,
    final_ref,
    slot_ref,
    mix_ref,
    faces_ref,
    send_ref,
    halo_ref,
    sems,
):
    fetch_halo(
        [recv_ref, relayed_ref, extra_ref], [FROM_B, FROM_G, FROM_X, FROM_X + 6], final_ref, halo_ref, sems
    )
    decoded = silu(coarse_halo(acc_ref, halo_ref, w_ref, coarse_edges()))
    dropped = dot3(up_ref[...], decoded)
    row = iota((128, 1024), 0)
    col = iota((128, 1024), 1)
    source = (col >> 9) * 64 + ((col >> 5) & 7) * 8 + ((col >> 1) & 7)
    widen = as01(source == row)
    for quad in range(4):
        wide = dot2(dropped[:, quad * 128 : (quad + 1) * 128], widen)
        at = slice(quad * 1024, (quad + 1) * 1024)
        mix_ref[:, at] = silu(first_ref[:, at] + wide)
    fine_faces(mix_ref, faces_ref)
    send_faces(faces_ref, send_ref, slot_ref, sems)


VMEM = pl.BlockSpec(memory_space=pltpu.VMEM)
SMEM = pl.BlockSpec(memory_space=pltpu.SMEM)
HBM = pl.BlockSpec(memory_space=pl.ANY)


def call(kernel, outs, args=(), pools=(), scalars=(), scratch=(), far=0):
    near = len(outs) - far
    return pl.pallas_call(
        kernel,
        out_shape=[jax.ShapeDtypeStruct(o, f32) for o in outs],
        in_specs=[VMEM] * len(args) + [HBM] * len(pools) + [SMEM] * len(scalars),
        out_specs=[VMEM] * near + [HBM] * far,
        scratch_shapes=list(scratch),
    )(*args, *pools, *scalars)


def route(scalars, sizes):
    return pl.pallas_call(
        route_kernel,
        out_shape=[jax.ShapeDtypeStruct((n,), jnp.int32) for n in sizes],
        in_specs=[SMEM] * len(scalars),
        out_specs=[SMEM] * len(sizes),
    )(*scalars)


def copy_sems(count):
    return pltpu.SemaphoreType.DMA((count,))


def dense_halo(faces, links):
    owners = lax.broadcasted_iota(jnp.int32, (BRICKS, 6), 0)
    chosen = links[None, :] == owners
    parcel = jnp.zeros((BRICKS, *faces.shape[1:]), f32)
    for face in range(6):
        parcel = jnp.where(chosen[:, face, None, None], faces[face][None], parcel)
    arrived = lax.all_to_all(parcel, ALL, 0, 0, tiled=True)
    halos = []
    for face in range(6):
        layer = lax.dynamic_index_in_dim(
            arrived, jnp.maximum(links[face], 0), 0, keepdims=False
        )
        halos.append(jnp.where(links[face] >= 0, layer, 0.0))
    return jnp.stack(halos)


def exchange(faces, send, relay, links, spilled):
    layer = faces.shape[1:]
    recv = lax.all_to_all(send, "brick", 0, 0, tiled=True)
    (onward,) = call(
        relay_kernel,
        [(GROUPS * SLOTS_G, *layer)],
        pools=[faces, recv],
        scalars=[relay],
        scratch=[copy_sems(GROUPS * SLOTS_G)],
        far=1,
    )
    arrived = lax.all_to_all(onward, "grp", 0, 0, tiled=True)
    extra = lax.cond(
        spilled, lambda v: dense_halo(v, links), lambda v: v, faces
    )
    return [recv, arrived, extra]


def overflows(table):
    rows = table.T
    bricks = lax.iota(jnp.int32, BRICKS)
    spilled = jnp.zeros((BRICKS,), jnp.bool_)
    for face in range(6):
        here = rows[face]
        same_b = jnp.zeros((BRICKS,), jnp.int32)
        same_g = jnp.zeros((BRICKS,), jnp.int32)
        for other in range(face):
            there = rows[other]
            same_b += ((there >= 0) & ((there & 15) == (here & 15))).astype(jnp.int32)
            same_g += ((there >= 0) & ((there >> 4) == (here >> 4))).astype(jnp.int32)
        valid = here >= 0
        over_b = valid & ((here & 15) != (bricks & 15)) & (same_b >= SLOTS_B)
        over_g = valid & ((here >> 4) != (bricks >> 4)) & (same_g >= SLOTS_G)
        spilled = spilled | over_b | over_g
    return jnp.any(spilled)


def per_device(
    noisy,
    neighbours,
    labels,
    conv_in,
    bias_in,
    down_fine,
    conv_mid,
    bias_mid,
    conv_res,
    conv_dec,
    down_mid,
    w_query,
    w_key,
    w_value,
    w_out,
    logit_scale,
    up_mid,
    up_fine,
    conv_out,
):
    links = neighbours[0]
    me = jnp.stack([lax.axis_index("grp"), lax.axis_index("brick")]).astype(jnp.int32)
    row = jnp.pad(links, (0, 122))
    rows = lax.all_to_all(
        jnp.broadcast_to(row[None], (BRICKS, 128)), ALL, 0, 0, tiled=True
    )
    table = rows[:, :6]
    spilled = overflows(table)
    slot, relay, final = route(
        [table.reshape(-1), me], [6, GROUPS * SLOTS_G, 6]
    )
    everything = jnp.where(links >= 0, FROM_X + lax.iota(jnp.int32, 6), -1)
    final = jnp.where(spilled, everything, final)

    def swap(faces, send):
        return exchange(faces, send, relay, links, spilled)

    def halo_scratch(rows, lanes):
        return [pltpu.VMEM((6, rows, lanes), f32), copy_sems(6)]

    fine_layer = (6, C1, 256)
    fine_send = (MEMBERS * SLOTS_B, C1, 256)
    layer = (6, C2 // 2, 128)
    layer_send = (MEMBERS * SLOTS_B, C2 // 2, 128)

    def fine_conv(v, w):
        return call(
            fine_conv_kernel,
            [(C1, S**3)],
            [v, w],
            scratch=[
                pltpu.VMEM((576, 4608), bf16),
                pltpu.VMEM((576, 4608), bf16),
                pltpu.VMEM((2 * C1, 27 * C1), bf16),
            ],
        )[0]

    def coarse_conv(v, w):
        return call(
            coarse_conv_kernel,
            [(C2, 512)],
            [v, w],
            scratch=[
                pltpu.VMEM((27 * C2, 512), bf16),
                pltpu.VMEM((27 * C2, 512), bf16),
                pltpu.VMEM((2 * C2, 27 * C2), bf16),
            ],
        )[0]

    fine_in = noisy[0]
    (faces,) = call(fine_face_kernel, [fine_layer], [fine_in])
    (send,) = call(
        pack_kernel, [fine_send], [faces], scalars=[slot], scratch=[copy_sems(6)], far=1
    )
    acc = fine_conv(fine_in, conv_in)
    pools = swap(faces, send)
    first, mid, send = call(
        fine_first_kernel,
        [(C1, S**3), (C2, 512), (BRICKS, C1 // 2, 128)],
        [acc, conv_in, bias_in[:, None], down_fine],
        pools,
        [final, links],
        [pltpu.VMEM(fine_layer, f32), pltpu.VMEM((6, C1 // 2, 128), f32), copy_sems(6)],
        far=1,
    )
    acc = coarse_conv(mid, conv_mid)
    arrived = lax.all_to_all(send, ALL, 0, 0, tiled=True)
    second, faces, send = call(
        second_kernel,
        [(C2, 512), layer, layer_send],
        [acc, conv_mid, bias_mid[:, None], down_fine],
        [arrived],
        [links, slot],
        halo_scratch(C1 // 2, 128),
        far=1,
    )
    acc = coarse_conv(second, conv_res)
    pools = swap(faces, send)
    refined, coarse = call(
        refined_kernel,
        [(C2, 512), (TOKB, C2)],
        [acc, conv_res, second],
        pools,
        [final],
        halo_scratch(C2 // 2, 128),
    )
    everyone = lax.all_to_all(
        jnp.broadcast_to(coarse[None], (MEMBERS, TOKB, C2)), "brick", 0, 0, tiled=True
    )
    joined, faces, send = call(
        attention_kernel,
        [(C2, 512), layer, layer_send],
        [
            everyone.reshape(MEMBERS * TOKB, C2),
            coarse,
            refined,
            down_mid,
            w_query,
            w_key,
            w_value,
            w_out,
            up_mid,
        ],
        [],
        [logit_scale, labels[0], me, slot],
        [copy_sems(6)],
        far=1,
    )
    acc = coarse_conv(joined, conv_dec)
    pools = swap(faces, send)
    mix, faces, send = call(
        decoded_kernel,
        [(C1, S**3), fine_layer, fine_send],
        [acc, conv_dec, up_fine, first],
        pools,
        [final, slot],
        halo_scratch(C2 // 2, 128),
        far=1,
    )
    acc = fine_conv(mix, conv_out)
    pools = swap(faces, send)
    (result,) = call(
        fine_last_kernel,
        [(C1, S**3)],
        [acc, conv_out],
        pools,
        [final],
        halo_scratch(C1, 256),
    )
    return result[None]


def solution(mesh):
    in_specs = (
        P(("grp", "brick"), None, None),
        P(("grp", "brick"), None),
        P("grp", None),
    ) + (P(),) * 16
    out_specs = P(("grp", "brick"), None, None)
    return jax.shard_map(
        per_device, mesh=mesh, in_specs=in_specs, out_specs=out_specs, check_vma=False
    )
```

time: 854 us -> 339 us (0.40); the launches traced: 840 us -> 343 us
  waiting for transfers between devices: 364 us -> 56.9 us
  local copies, waits for them, and re-layouts: 265 us -> 16.4 us
  matrix products: 159 us -> 0 us
  blocking collectives: 0 us -> 111 us
  Pallas kernels: 0 us -> 102 us
    all_to_all x6, waiting for transfers between devices: 364 us -> 56.9 us  [the longest x4 27.2 us: exchange(): arrived = lax.all_to_all(onward, 'grp', 0, 0, tiled=True)]
    dot_general x35 -> x0, matrix products: 159 us -> none  [the longest x15 102 us: convolve(): jnp.dot(weight_part, stacked, precision=HIGHEST, preferred_element_type=j...]
    all_to_all x0 -> x5, blocking collectives: none -> 111 us  [the longest x4 97.4 us: exchange(): recv = lax.all_to_all(send, 'brick', 0, 0, tiled=True)]
    pallas_call x0 -> x18, Pallas kernels: none -> 102 us  [the longest x17 99.5 us: call(): pl.pallas_call(kernel, out_shape=[jax.ShapeDtypeStruct(o, f32) for o in o...]
    concatenate x15 -> x0, local copies, waits for them, and re-layouts: 97.7 us -> none  [convolve(): stacked = jnp.concatenate(shifted, axis=0)]
    slice x42 -> x0, local copies, waits for them, and re-layouts: 76.5 us -> none  [the longest x10 73.7 us: convolve(): padded[:, along_x:along_x + edge_len, along_y:along_y + edge_len, along_z...]
    scatter x30 -> x0, local copies, waits for them, and re-layouts: 34.3 us -> none  [the longest x5 9.86 us: padded_block(): padded = padded.at[:, 1:-1, 1:-1, -1].set(sheets[5])]
    dot_general x6 -> x0, local copies, waits for them, and re-layouts: 30.1 us -> none  [the longest x5 30 us: fetch_halo(): parcel = jnp.einsum('ng,gcv->ncv', outgoing, face_sheets, precision=HIGHEST)]
  transfers between devices with their start and end apart: 6 -> 6, of which waited for: 6 -> 6; matrix products, arithmetic and copies ran while one was open for 1% -> 1% of each run, Pallas kernels for 0% -> 13%
where the time goes in v1:
time: 339 us; the launch traced here: 343 us
  blocking collectives  111 us (33%)
  Pallas kernels  102 us (30%)
  waiting for transfers between devices  56.9 us (17%)
  starting transfers between devices  52.1 us (15%)
  local copies, waits for them, and re-layouts  16.4 us (5%)
    pallas_call x17, Pallas kernels, call(): pl.pallas_call(kernel, out_shape=[jax.ShapeDtypeStruct(o, f32) for o in o...  99.5 us
    all_to_all x4, blocking collectives, exchange(): recv = lax.all_to_all(send, 'brick', 0, 0, tiled=True)  97.4 us
    all_to_all x4, starting transfers between devices, exchange(): arrived = lax.all_to_all(onward, 'grp', 0, 0, tiled=True)  36.2 us
    all_to_all x4, waiting for transfers between devices, exchange(): arrived = lax.all_to_all(onward, 'grp', 0, 0, tiled=True)  27.2 us
    all_to_all x1, waiting for transfers between devices, per_device(): arrived = lax.all_to_all(send, ALL, 0, 0, tiled=True)  22.6 us
    all_to_all x1, blocking collectives, per_device(): lax.all_to_all(jnp.broadcast_to(coarse[None], (MEMBERS, TOKB, C2)), 'bric...  13.7 us
    all_to_all x1, starting transfers between devices, per_device(): lax.all_to_all(jnp.broadcast_to(row[None], (BRICKS, 128)), ALL, 0, 0, til...  11.5 us
    unnamed x29, local copies, waits for them, and re-layouts  9.24 us
  transfers between devices with their start and end apart: 6, of which 6 were waited for; matrix products, arithmetic and copies ran while one was open for 1% of the time, Pallas kernels for 13%

profile of v1, /device:TPU:1, one launch (start us, length us, event | category | flops | bytes accessed | tf_op | source)
XLA Modules:
  0.0 342.7 jit_solution(2507503030640118215)
XLA Ops:
  1.3 11.5 %all-to-all-start.4 = ((s32[128,1,128]{2,1,0:T(1,128)}), s32[128,1,128]{2,1,0:T(1,128)S(1)}, u32[]{:S(2)}, u32[]{:S(2)}) async-start(s32[128,1,128]{2,1,0:T(1,128)} %broadcast_in_dim.408), calls=%async_computation.4 | async-start | bytes 131072 | tf_op jit(solution)/shard_map/all_to_all | solution.py:764
  15.2 7.2 %all-to-all-done.4 = s32[128,1,128]{2,1,0:T(1,128)S(1)} async-done(((s32[128,1,128]{2,1,0:T(1,128)}), s32[128,1,128]{2,1,0:T(1,128)S(1)}, u32[]{:S(2)}, u32[]{:S(2)}) %all-to-all-start.4) | async-done | bytes 65568 | tf_op jit(solution)/shard_map/all_to_all | solution.py:764
  30.6 30.5 %all_to_all.75.recv_ref = f32[32,64,256]{2,1,0:T(8,128)} all-to-all(f32[32,64,256]{2,1,0:T(8,128)S(1)} %copy-done.1), channel_id=1, replica_groups=mesh['grp'=8,'brick'=16] {'brick'}, dimensions={0} | all-to-all | bytes 4194304 | tf_op jit(solution)/shard_map/all_to_all | solution.py:705
  65.3 9.4 %all-to-all-start.6 = ((f32[24,64,256]{2,1,0:T(8,128)}), f32[24,64,256]{2,1,0:T(8,128)S(1)}, u32[]{:S(2)}, u32[]{:S(2)}) async-start(f32[24,64,256]{2,1,0:T(8,128)} %shard_map.185), calls=%async_computation.6 | async-start | bytes 3145728 | tf_op jit(solution)/shard_map/all_to_all | solution.py:714
  74.8 11.3 %shard_map.181.acc_ref = f32[64,4096]{1,0:T(8,128)} custom-call(f32[64,4096]{1,0:T(8,128)} %bitcast.162, f32[64,1728]{1,0:T(8,128)} %w_ref.11), custom_call_target="tpu_custom_call" | custom-call | tf_op jit(solution)/shard_map/pallas_call | solution.py:665
  88.7 6.6 %all-to-all-done.6.relayed_ref = f32[24,64,256]{2,1,0:T(8,128)S(1)} async-done(((f32[24,64,256]{2,1,0:T(8,128)}), f32[24,64,256]{2,1,0:T(8,128)S(1)}, u32[]{:S(2)}, u32[]{:S(2)}) %all-to-all-start.6) | async-done | bytes 1572896 | tf_op jit(solution)/shard_map/all_to_all | solution.py:714
  96.5 6.9 %shard_map.186 = (f32[64,4096]{1,0:T(8,128)}, f32[128,512]{1,0:T(8,128)}, f32[128,32,128]{2,1,0:T(8,128)}) custom-call(f32[64,4096]{1,0:T(8,128)} %shard_map.181.acc_ref, f32[64,1728]{1,0:T(8,128)} %w_ref.11, f32[64,1]{1,0:T(8,128)} %copy.33.bias_ref, f32[128,64]{1,0:T(8,128)} %copy.34.down_ref, f32[32,64,256]{2,1,0:T(8,128)} %all_to_all.75.recv_ref, ...), custom_call_target="tpu_custom_call" | custom-call | tf_op jit(solution)/shard_map/pallas_call | solution.py:665
  108.6 6.6 %shard_map.187.acc_ref = f32[128,512]{1,0:T(8,128)} custom-call(f32[128,512]{1,0:T(8,128)} %get-tuple-element.77.v_ref, f32[128,3456]{1,0:T(8,128)} %w_ref.13), custom_call_target="tpu_custom_call" | custom-call | tf_op jit(solution)/shard_map/pallas_call | solution.py:665
  115.2 22.6 %all-to-all-done.7.arrived_ref = f32[128,32,128]{2,1,0:T(8,128)S(1)} async-done(((f32[128,32,128]{2,1,0:T(8,128)}), f32[128,32,128]{2,1,0:T(8,128)S(1)}, u32[]{:S(2)}, u32[]{:S(2)}) %all-to-all-start.7) | async-done | bytes 2097184 | tf_op jit(solution)/shard_map/all_to_all | solution.py:827
  139.1 6.7 %shard_map.188 = (f32[128,512]{1,0:T(8,128)}, f32[6,64,128]{2,1,0:T(8,128)S(1)}, f32[32,64,128]{2,1,0:T(8,128)}) custom-call(f32[128,512]{1,0:T(8,128)} %shard_map.187.acc_ref, f32[128,3456]{1,0:T(8,128)} %w_ref.13, f32[128,1]{1,0:T(8,128)} %copy.35.bias_ref, f32[128,64]{1,0:T(8,128)} %copy.34.down_ref, f32[128,32,128]{2,1,0:T(8,128)} %copy-done, ...), custom_call_target="tpu_custom_call" | custom-call | tf_op jit(solution)/shard_map/pallas_call | solution.py:665
  147.1 18.1 %all_to_all.76.recv_ref = f32[32,64,128]{2,1,0:T(8,128)} all-to-all(f32[32,64,128]{2,1,0:T(8,128)S(1)} %copy-done.7), channel_id=1, replica_groups=mesh['grp'=8,'brick'=16] {'brick'}, dimensions={0} | all-to-all | bytes 2097152 | tf_op jit(solution)/shard_map/all_to_all | solution.py:705
  168.2 8.9 %all-to-all-start.9 = ((f32[24,64,128]{2,1,0:T(8,128)}), f32[24,64,128]{2,1,0:T(8,128)S(1)}, u32[]{:S(2)}, u32[]{:S(2)}) async-start(f32[24,64,128]{2,1,0:T(8,128)} %shard_map.190), calls=%async_computation.9 | async-start | bytes 1572864 | tf_op jit(solution)/shard_map/all_to_all | solution.py:714
  177.1 6.6 %shard_map.189.acc_ref = f32[128,512]{1,0:T(8,128)} custom-call(f32[128,512]{1,0:T(8,128)} %get-tuple-element.79.v_ref.second_ref, f32[128,3456]{1,0:T(8,128)} %w_ref.15), custom_call_target="tpu_custom_call" | custom-call | tf_op jit(solution)/shard_map/pallas_call | solution.py:665
  183.6 5.6 %all-to-all-done.9.relayed_ref = f32[24,64,128]{2,1,0:T(8,128)S(1)} async-done(((f32[24,64,128]{2,1,0:T(8,128)}), f32[24,64,128]{2,1,0:T(8,128)S(1)}, u32[]{:S(2)}, u32[]{:S(2)}) %all-to-all-start.9) | async-done | bytes 786464 | tf_op jit(solution)/shard_map/all_to_all | solution.py:714
  196.4 13.7 %all_to_all.77 = f32[16,64,128]{2,1,0:T(8,128)} all-to-all(f32[16,64,128]{2,1,0:T(8,128)S(1)} %broadcast_in_dim.411), channel_id=1, replica_groups=mesh['grp'=8,'brick'=16] {'brick'}, dimensions={0} | all-to-all | bytes 1048576 | tf_op jit(solution)/shard_map/all_to_all | solution.py:847
  210.1 8.1 %shard_map.192 = (f32[128,512]{1,0:T(8,128)}, f32[6,64,128]{2,1,0:T(8,128)S(1)}, f32[32,64,128]{2,1,0:T(8,128)}) custom-call(f32[1024,128]{1,0:T(8,128)} %bitcast.163, f32[64,128]{1,0:T(8,128)} %get-tuple-element.82.own_ref, f32[128,512]{1,0:T(8,128)} %get-tuple-element.83.refined_ref, f32[256,128]{1,0:T(8,128)} %down_ref.3, f32[256,256]{1,0:T(8,128)} %wq_ref.1, ...), custom_call_target="tpu_custom_call" | custom-call | tf_op jit(solution)/shard_map/pallas_call | solution.py:665
  219.4 18.3 %all_to_all.78.recv_ref = f32[32,64,128]{2,1,0:T(8,128)} all-to-all(f32[32,64,128]{2,1,0:T(8,128)S(1)} %copy-done.8), channel_id=1, replica_groups=mesh['grp'=8,'brick'=16] {'brick'}, dimensions={0} | all-to-all | bytes 2097152 | tf_op jit(solution)/shard_map/all_to_all | solution.py:705
  240.8 8.5 %all-to-all-start.12 = ((f32[24,64,128]{2,1,0:T(8,128)}), f32[24,64,128]{2,1,0:T(8,128)S(1)}, u32[]{:S(2)}, u32[]{:S(2)}) async-start(f32[24,64,128]{2,1,0:T(8,128)} %shard_map.194), calls=%async_computation.12 | async-start | bytes 1572864 | tf_op jit(solution)/shard_map/all_to_all | solution.py:714
  249.3 6.6 %shard_map.193.acc_ref = f32[128,512]{1,0:T(8,128)} custom-call(f32[128,512]{1,0:T(8,128)} %get-tuple-element.84.v_ref, f32[128,3456]{1,0:T(8,128)} %w_ref.17), custom_call_target="tpu_custom_call" | custom-call | tf_op jit(solution)/shard_map/pallas_call | solution.py:665
  262.3 7.6 %shard_map.195 = (f32[64,4096]{1,0:T(8,128)}, f32[6,64,256]{2,1,0:T(8,128)S(1)}, f32[32,64,256]{2,1,0:T(8,128)}) custom-call(f32[128,512]{1,0:T(8,128)} %shard_map.193.acc_ref, f32[128,3456]{1,0:T(8,128)} %w_ref.17, f32[64,128]{1,0:T(8,128)} %up_ref.3, f32[64,4096]{1,0:T(8,128)} %get-tuple-element.85.first_ref, f32[32,64,128]{2,1,0:T(8,128)} %all_to_all.78.recv_ref, ...), custom_call_target="tpu_custom_call" | custom-call | tf_op jit(solution)/shard_map/pallas_call | solution.py:665
  271.7 30.5 %all_to_all.79.recv_ref = f32[32,64,256]{2,1,0:T(8,128)} all-to-all(f32[32,64,256]{2,1,0:T(8,128)S(1)} %copy-done.6), channel_id=1, replica_groups=mesh['grp'=8,'brick'=16] {'brick'}, dimensions={0} | all-to-all | bytes 4194304 | tf_op jit(solution)/shard_map/all_to_all | solution.py:705
  306.2 9.4 %all-to-all-start.14 = ((f32[24,64,256]{2,1,0:T(8,128)}), f32[24,64,256]{2,1,0:T(8,128)S(1)}, u32[]{:S(2)}, u32[]{:S(2)}) async-start(f32[24,64,256]{2,1,0:T(8,128)} %shard_map.197), calls=%async_computation.14 | async-start | bytes 3145728 | tf_op jit(solution)/shard_map/all_to_all | solution.py:714
  315.7 11.3 %shard_map.196.acc_ref = f32[64,4096]{1,0:T(8,128)} custom-call(f32[64,4096]{1,0:T(8,128)} %get-tuple-element.88.v_ref, f32[64,1728]{1,0:T(8,128)} %w_ref.19), custom_call_target="tpu_custom_call" | custom-call | tf_op jit(solution)/shard_map/pallas_call | solution.py:665
  327.0 9.3 %all-to-all-done.14.relayed_ref = f32[24,64,256]{2,1,0:T(8,128)S(1)} async-done(((f32[24,64,256]{2,1,0:T(8,128)}), f32[24,64,256]{2,1,0:T(8,128)S(1)}, u32[]{:S(2)}, u32[]{:S(2)}) %all-to-all-start.14) | async-done | bytes 1572896 | tf_op jit(solution)/shard_map/all_to_all | solution.py:714
  (60 shorter events, 62.8 us)
Async XLA Ops:
  1.3 21.0 %all-to-all-start.4 = ((s32[128,1,128]{2,1,0:T(1,128)}), s32[128,1,128]{2,1,0:T(1,128)S(1)}, u32[]{:S(2)}, u32[]{:S(2)}) async-start(s32[128,1,128]{2,1,0:T(1,128)} %broadcast_in_dim.408), calls=%async_computation.4 | async-start | bytes 131072 | tf_op jit(solution)/shard_map/all_to_all | solution.py:764
  28.9 1.7 copy-start.1
  61.1 24.9 %copy-start.11 = (f32[128,64]{0,1:T(8,128)S(1)}, f32[128,64]{0,1:T(8,128)}, u32[]{:S(2)}) copy-start(f32[128,64]{0,1:T(8,128)} %param.32) | copy-start | bytes 98308
  61.1 25.6 %copy-start.12 = (f32[64]{0:T(128)S(1)}, f32[64]{0:T(128)}, u32[]{:S(2)}) copy-start(f32[64]{0:T(128)} %param.31) | copy-start | bytes 772
  61.1 26.3 %copy-start.9 = (s32[1,6]{1,0:T(1,128)S(1)}, s32[1,6]{1,0:T(1,128)}, u32[]{:S(2)}) copy-start(s32[1,6]{1,0:T(1,128)} %param.28) | copy-start | bytes 76
  61.1 26.3 %copy-start.14 = (s32[6]{0:T(128)S(1)}, s32[6]{0:T(128)}, u32[]{:S(2)}) copy-start(s32[6]{0:T(128)} %get-tuple-element.76) | copy-start | bytes 76
  65.3 30.1 %all-to-all-start.6 = ((f32[24,64,256]{2,1,0:T(8,128)}), f32[24,64,256]{2,1,0:T(8,128)S(1)}, u32[]{:S(2)}, u32[]{:S(2)}) async-start(f32[24,64,256]{2,1,0:T(8,128)} %shard_map.185), calls=%async_computation.6 | async-start | bytes 3145728 | tf_op jit(solution)/shard_map/all_to_all | solution.py:714
  88.7 19.1 %copy-start.13 = (f32[128]{0:T(128)S(1)}, f32[128]{0:T(128)}, u32[]{:S(2)}) copy-start(f32[128]{0:T(128)} %param.34) | copy-start | bytes 1540
  95.4 1.2 copy-start.2
  103.4 34.3 %all-to-all-start.7 = ((f32[128,32,128]{2,1,0:T(8,128)}), f32[128,32,128]{2,1,0:T(8,128)S(1)}, u32[]{:S(2)}, u32[]{:S(2)}) async-start(f32[128,32,128]{2,1,0:T(8,128)} %get-tuple-element.78), calls=%async_computation.7 | async-start | bytes 4194304 | tf_op jit(solution)/shard_map/all_to_all | solution.py:827
  137.7 1.3 copy-start
  145.8 1.3 copy-start.7
  168.2 21.0 %all-to-all-start.9 = ((f32[24,64,128]{2,1,0:T(8,128)}), f32[24,64,128]{2,1,0:T(8,128)S(1)}, u32[]{:S(2)}, u32[]{:S(2)}) async-start(f32[24,64,128]{2,1,0:T(8,128)} %shard_map.190), calls=%async_computation.9 | async-start | bytes 1572864 | tf_op jit(solution)/shard_map/all_to_all | solution.py:714
  189.3 0.9 copy-start.4
  218.1 1.3 copy-start.8
  240.8 20.7 %all-to-all-start.12 = ((f32[24,64,128]{2,1,0:T(8,128)}), f32[24,64,128]{2,1,0:T(8,128)S(1)}, u32[]{:S(2)}, u32[]{:S(2)}) async-start(f32[24,64,128]{2,1,0:T(8,128)} %shard_map.194), calls=%async_computation.12 | async-start | bytes 1572864 | tf_op jit(solution)/shard_map/all_to_all | solution.py:714
  261.4 0.9 copy-start.5
  270.0 1.7 copy-start.6
  306.2 30.1 %all-to-all-start.14 = ((f32[24,64,256]{2,1,0:T(8,128)}), f32[24,64,256]{2,1,0:T(8,128)S(1)}, u32[]{:S(2)}, u32[]{:S(2)}) async-start(f32[24,64,256]{2,1,0:T(8,128)} %shard_map.197), calls=%async_computation.14 | async-start | bytes 3145728 | tf_op jit(solution)/shard_map/all_to_all | solution.py:714
  336.3 1.1 copy-start.3
